TPU v7x, 32 devices: a whole 2x2x4 slice. The times are simulated.
32 devices in a mesh: member: 2 (over y), slab: 4 (over z), chan: 2 (over x), mode: 2 (over core).
Axes of the slice: x: 2, y: 2, z: 4, core: 2. Of those that a mesh axis runs over, the one named last changes fastest.
Arguments:
- source_field: float32 [128, 1024, 1024], P(('member', 'chan'), 'slab', 'mode'), parts along dimension 0, may hold values from -6 to 6
- cotangent: float32 [128, 1024, 1024], P(('member', 'chan'), 'slab', 'mode'), parts along dimension 0, may hold values from -6 to 6
- spectral_weight: float32 [128, 64, 32, 2, 64], P(('member', 'chan'), None, 'mode', None, 'slab'), parts along dimension 0, may hold values from -12 to 12
- skip_gain: float32 [128], P(('member', 'chan')), parts along dimension 0, may hold values from 0.5 to 2
- channel_bias: float32 [128], P(('member', 'chan')), parts along dimension 0, may hold values from -0.5 to 0.5
- mode_limit: int32 [128, 2], P('member'), parts along dimension 0, may hold values from 16 to 32
- width_limit: int32 [128], P('member'), parts along dimension 0, may hold values from 32 to 64
Outputs:
- output: float32 [128, 1024, 1024], P(('member', 'chan'), 'slab', 'mode'), parts along dimension 0
- field_grad: float32 [128, 1024, 1024], P(('member', 'chan'), 'slab', 'mode'), parts along dimension 0
- spectral_grad: float32 [128, 64, 32, 2, 64], P(('member', 'chan'), None, 'mode', None, 'slab'), parts along dimension 0
- gate_grad: float32 [128], P(('member', 'chan')), parts along dimension 0
- bias_grad: float32 [128], P(('member', 'chan')), parts along dimension 0
There are 2 independent parts, one for each index of `member`. A program takes and returns all parts, laid end to end along the dimension named above; each array names one. Nothing has to cross between parts.
Inputs may be any that keep to these rules, and one draw needn't show every extreme that they name: `mode_limit`: never more than 32. `width_limit`: never more than 64.
All inputs are finite; a program needn't handle non-finite values.
Results may differ from a plain program's by a relative error of at most 0.00018.
Values sent between devices are 32-bit elements; how exact they have to be, the bound alone decides.
No kernel may reach another device: no remote copies, remote signals or barrier semaphores. Data moves between devices by JAX's collectives and lax.ppermute only.
A program may use at most 192 MiB of HBM per device.

v0:
```python
import math
import jax
import jax.numpy as jnp
from jax import lax
from jax.sharding import PartitionSpec as P

precise = lax.Precision.HIGHEST


def column_table(extent, freq_count, first_cell, cell_count):
    cell_index = first_cell + jnp.arange(cell_count, dtype=jnp.int32)
    wave_index = jnp.arange(freq_count, dtype=jnp.int32)
    products = (cell_index[:, None] * wave_index[None, :] % extent).astype(jnp.float32)
    angles = products * (2.0 * math.pi / extent)
    return jnp.stack([jnp.cos(angles), -jnp.sin(angles)], axis=-1).reshape(
        cell_count, 2 * freq_count
    )


def row_tables(extent, freq_count, first_cell, cell_count):
    cell_index = first_cell + jnp.arange(cell_count, dtype=jnp.int32)
    column = jnp.arange(2 * freq_count, dtype=jnp.int32)
    wave_index = column + jnp.where(column >= freq_count, extent - 2 * freq_count, 0)
    products = (cell_index[:, None] * wave_index[None, :] % extent).astype(jnp.float32)
    angles = products * (2.0 * math.pi / extent)
    return (jnp.cos(angles), jnp.sin(angles))


def row_forward(lined, row_cos, row_sin):
    line_real = lined[:, 0]
    line_imag = lined[:, 1]
    out_real = jnp.dot(line_real, row_cos, precision=precise) + jnp.dot(
        line_imag, row_sin, precision=precise
    )
    out_imag = jnp.dot(line_imag, row_cos, precision=precise) - jnp.dot(
        line_real, row_sin, precision=precise
    )
    return jnp.stack([out_real, out_imag], axis=1)


def row_inverse(modes_in, row_cos, row_sin):
    mode_real = modes_in[:, 0]
    mode_imag = modes_in[:, 1]
    back_real = jnp.dot(mode_real, row_cos.T, precision=precise) - jnp.dot(
        mode_imag, row_sin.T, precision=precise
    )
    back_imag = jnp.dot(mode_real, row_sin.T, precision=precise) + jnp.dot(
        mode_imag, row_cos.T, precision=precise
    )
    return jnp.stack([back_real, back_imag], axis=1)


def contract(spectra, weight):
    spec_real = spectra[:, :, 0]
    spec_imag = spectra[:, :, 1]
    weight_real = weight[:, :, :, 0]
    weight_imag = weight[:, :, :, 1]
    out_real = jnp.einsum("iyx,ioyx->oyx", spec_real, weight_real, precision=precise) - jnp.einsum(
        "iyx,ioyx->oyx", spec_imag, weight_imag, precision=precise
    )
    out_imag = jnp.einsum("iyx,ioyx->oyx", spec_real, weight_imag, precision=precise) + jnp.einsum(
        "iyx,ioyx->oyx", spec_imag, weight_real, precision=precise
    )
    return jnp.stack([out_real, out_imag], axis=2)


def contract_back(grads, weight):
    grad_real = grads[:, :, 0]
    grad_imag = grads[:, :, 1]
    weight_real = weight[:, :, :, 0]
    weight_imag = weight[:, :, :, 1]
    back_real = jnp.einsum("oyx,ioyx->iyx", grad_real, weight_real, precision=precise) + jnp.einsum(
        "oyx,ioyx->iyx", grad_imag, weight_imag, precision=precise
    )
    back_imag = jnp.einsum("oyx,ioyx->iyx", grad_imag, weight_real, precision=precise) - jnp.einsum(
        "oyx,ioyx->iyx", grad_real, weight_imag, precision=precise
    )
    return jnp.stack([back_real, back_imag], axis=2)


def outer_grad(spectra, grads):
    spec_real = spectra[:, :, 0]
    spec_imag = spectra[:, :, 1]
    grad_real = grads[:, :, 0]
    grad_imag = grads[:, :, 1]
    real_side = jnp.einsum("iyx,oyx->ioyx", spec_real, grad_real) + jnp.einsum(
        "iyx,oyx->ioyx", spec_imag, grad_imag
    )
    imag_side = jnp.einsum("iyx,oyx->ioyx", spec_real, grad_imag) - jnp.einsum(
        "iyx,oyx->ioyx", spec_imag, grad_real
    )
    return jnp.stack([real_side, imag_side], axis=3)


def mode_weights(limit_rows, col_freq, row_freq, kx_count, cells_total):
    keep_cols = col_freq[None, :] < limit_rows[:, 0:1]
    keep_rows = (row_freq[None, :] < limit_rows[:, 1:2]) | (
        (kx_count - row_freq)[None, :] < limit_rows[:, 1:2]
    )
    scales = jnp.where(col_freq == 0, 1.0, 2.0).astype(jnp.float32) / cells_total
    joined = keep_cols[:, :, None] & keep_rows[:, None, :]
    return (joined.astype(jnp.float32) * scales[None, :, None])[:, :, None, :]


def read_mask(in_index, width_limit):
    return (in_index[:, None] < width_limit[None, :]).astype(jnp.float32)[:, :, None, None, None]


def local(
    source_field, cotangent, spectral_weight, skip_gain, channel_bias, mode_limit, width_limit
):
    channels, row_count, col_count = source_field.shape
    slab_count = lax.axis_size("slab")
    mode_count = lax.axis_size("mode")
    slab_index = lax.axis_index("slab")
    mode_index = lax.axis_index("mode")
    chan_index = lax.axis_index("chan")
    local_freq = spectral_weight.shape[2]
    local_kx = spectral_weight.shape[4]
    freq_count = local_freq * mode_count
    kx_count = local_kx * slab_count
    all_rows = row_count * slab_count
    all_cols = col_count * mode_count
    column_tab = column_table(all_cols, freq_count, mode_index * col_count, col_count)
    row_cos, row_sin = row_tables(all_rows, freq_count, slab_index * row_count, row_count)

    def spectrum(values):
        partial_cols = jnp.einsum("chw,wk->ckh", values, column_tab, precision=precise)
        summed_cols = lax.psum_scatter(partial_cols, "mode", scatter_dimension=1, tiled=True)
        paired = summed_cols.reshape(values.shape[0] * local_freq, 2, row_count)
        spectra = lax.psum_scatter(
            row_forward(paired, row_cos, row_sin), "slab", scatter_dimension=2, tiled=True
        )
        return spectra.reshape(values.shape[0], local_freq, 2, local_kx)

    def synthesis(modes_in):
        whole_modes = lax.all_gather(modes_in, "slab", axis=3, tiled=True)
        rebuilt = row_inverse(
            whole_modes.reshape(channels * local_freq, 2, kx_count), row_cos, row_sin
        )
        rebuilt = rebuilt.reshape(channels, 2 * local_freq, row_count)
        gathered = lax.all_gather(rebuilt, "mode", axis=1, tiled=True)
        return jnp.einsum("ckh,wk->chw", gathered, column_tab, precision=precise)

    in_index = chan_index * channels + jnp.arange(channels, dtype=jnp.int32)
    col_freq = mode_index * local_freq + jnp.arange(local_freq, dtype=jnp.int32)
    row_freq = slab_index * local_kx + jnp.arange(local_kx, dtype=jnp.int32)
    limit_rows = lax.dynamic_slice_in_dim(mode_limit, chan_index * channels, channels, 0)
    weights = mode_weights(limit_rows, col_freq, row_freq, kx_count, all_rows * all_cols)
    reads = read_mask(in_index, width_limit)
    masked_weight = spectral_weight * reads
    spectra = spectrum(source_field)
    out_modes = (
        lax.psum_scatter(contract(spectra, masked_weight), "chan", scatter_dimension=0, tiled=True)
        * weights
    )
    branch = synthesis(out_modes)
    skip_scale = skip_gain[:, None, None]
    summed = branch + skip_scale * source_field + channel_bias[:, None, None]
    output, gelu_back = jax.vjp(jax.nn.gelu, summed)
    grad_sum = gelu_back(cotangent)[0]
    grad_modes = spectrum(grad_sum) * weights
    all_grads = lax.all_gather(grad_modes, "chan", axis=0, tiled=True)
    spectral_grad = outer_grad(spectra, all_grads) * reads
    field_grad = synthesis(contract_back(all_grads, masked_weight)) + skip_scale * grad_sum
    gate_grad, bias_grad = lax.psum(
        (jnp.sum(grad_sum * source_field, axis=(1, 2)), jnp.sum(grad_sum, axis=(1, 2))),
        ("slab", "mode"),
    )
    return (output, field_grad, spectral_grad, gate_grad, bias_grad)


def solution(mesh):
    in_specs = (
        P(("member", "chan"), "slab", "mode"),
        P(("member", "chan"), "slab", "mode"),
        P(("member", "chan"), None, "mode", None, "slab"),
        P(("member", "chan")),
        P(("member", "chan")),
        P("member", None),
        P("member"),
    )
    out_specs = (
        P(("member", "chan"), "slab", "mode"),
        P(("member", "chan"), "slab", "mode"),
        P(("member", "chan"), None, "mode", None, "slab"),
        P(("member", "chan")),
        P(("member", "chan")),
    )
    return jax.shard_map(local, mesh=mesh, in_specs=in_specs, out_specs=out_specs, check_vma=False)
```

profile of v0, /device:TPU:0, one launch (start us, length us, event | category | flops | bytes accessed | tf_op | source)
XLA Modules:
  0.0 418.1 jit_solution(5773580187036393755)
XLA Ops:
  7.8 20.7 %convolution_bitcast_fusion.1 = f32[32,64,256]{2,1,0:T(8,128)} fusion(f32[512,64,1]{0,1,2:T(8,128)S(1)} %reshape.294, f32[32,256,512]{2,1,0:T(8,128)} %param.7), kind=kOutput, calls=%fused_computation.35 | convolution fusion | flops 3221225472 | bytes 19005440 | tf_op jit(solution)/shard_map/chw,wk->ckh/dot_general | solution.py:128
  29.8 8.5 %broadcast_multiply_fusion = f32[32,64,16,2,16]{1,4,3,2,0:T(8,128)} fusion(f32[32,64,16,2,16]{1,4,3,2,0:T(8,128)} %param.9, f32[32,64]{1,0:T(8,128)S(1)} %compare_convert_fusion), kind=kLoop, calls=%fused_computation.17 | loop fusion | flops 1048576 | bytes 8396800 | tf_op jit(solution)/shard_map/mul | solution.py:151
  38.3 2.7 reduce-scatter.6.cloned.1.call-done
  41.0 1.8 reshape.286
  49.5 7.8 %slice_bitcast_fusion.1 = (f32[32,64,16,16]{1,3,2,0:T(8,128)}, f32[32,64,16,16]{1,3,2,0:T(8,128)}) fusion(f32[32,64,16,2,16]{1,4,3,2,0:T(8,128)} %broadcast_multiply_fusion), kind=kLoop, calls=%fused_computation.14 | loop fusion | bytes 8388608 | tf_op jit(solution)/shard_map/squeeze | solution.py:56
  57.3 13.4 %reduce-scatter.8.cloned.1.call-done = f32[512,2,16]{0,2,1:T(8,128)} async-done(((f32[512,2,64]{0,2,1:T(8,128)}), f32[512,2,16]{0,2,1:T(8,128)}) %reduce-scatter.8.cloned.1.call-update) | async-done | bytes 65552 | tf_op jit(solution)/shard_map/reduce_scatter | solution.py:131
  72.1 8.3 %fusion.18 = f32[16,16,1,64]{3,2,1,0:T(1,128)S(1)} fusion(f32[32,16,16,1]{0,3,2,1:T(1,128)S(1)} %copy.60, f32[32,64,16,16]{1,3,2,0:T(8,128)} %get-tuple-element.11), kind=kOutput, calls=%fused_computation.30 | convolution fusion | flops 6291456 | bytes 2195456 | tf_op jit(solution)/shard_map/iyx,ioyx->oyx/dot_general | solution.py:61
  80.5 8.6 %fusion.12 = f32[16,16,1,64]{3,2,1,0:T(1,128)S(1)} fusion(f32[32,16,16,1]{0,3,2,1:T(1,128)S(1)} %copy.60, f32[32,64,16,16]{1,3,2,0:T(8,128)} %get-tuple-element.12), kind=kOutput, calls=%fused_computation.24 | convolution fusion | flops 6291456 | bytes 2195456 | tf_op jit(solution)/shard_map/iyx,ioyx->oyx/dot_general | solution.py:58
  89.1 6.0 %fusion.20 = f32[16,16,1,64]{3,2,1,0:T(1,128)S(1)} fusion(f32[32,16,16,1]{0,3,2,1:T(1,128)S(1)} %copy.57, f32[32,64,16,16]{1,3,2,0:T(8,128)S(1)} %copy-done.3), kind=kOutput, calls=%fused_computation.32 | convolution fusion | flops 6291456 | bytes 2195456 | tf_op jit(solution)/shard_map/iyx,ioyx->oyx/dot_general | solution.py:58
  95.2 6.2 %fusion.10 = f32[16,16,1,64]{3,2,1,0:T(1,128)S(1)} fusion(f32[32,16,16,1]{0,3,2,1:T(1,128)S(1)} %copy.57, f32[32,64,16,16]{1,3,2,0:T(8,128)S(1)} %copy-done.2), kind=kOutput, calls=%fused_computation.22 | convolution fusion | flops 6291456 | bytes 2195456 | tf_op jit(solution)/shard_map/iyx,ioyx->oyx/dot_general | solution.py:61
  101.5 1.3 copy.46
  103.0 18.5 %reduce-scatter.10.cloned.1.call-done = f32[32,16,2,16]{1,0,3,2:T(8,128)} async-done(((f32[64,16,2,16]{1,0,3,2:T(8,128)}), f32[32,16,2,16]{1,0,3,2:T(8,128)}) %reduce-scatter.10.cloned.1.call-update) | async-done | bytes 65552 | tf_op jit(solution)/shard_map/reduce_scatter | solution.py:154
  122.7 38.4 %all_gather.15 = f32[32,16,2,64]{1,0,3,2:T(8,128)S(1)} all-gather(f32[32,16,2,16]{1,0,3,2:T(8,128)S(1)} %broadcast_multiply_fusion.2), channel_id=1, replica_groups=mesh['member'=2,'slab'=4,'chan'=2,'mode'=2] {'slab'}, dimensions={3}, use_global_device_ids=true | all-gather | bytes 327680 | tf_op jit(solution)/shard_map/all_gather | solution.py:137
  167.9 1.7 reshape.289
  169.7 11.1 %all-gather.3.cloned.1.call-done = f32[32,64,256]{2,1,0:T(8,128)} async-done(((f32[32,32,256]{2,1,0:T(8,128)}), f32[32,64,256]{2,1,0:T(8,128)}) %all-gather.3.cloned.1.call-update) | async-done | bytes 2097168 | tf_op jit(solution)/shard_map/all_gather | solution.py:142
  180.9 36.1 %fusion.150 = (f32[32]{0:T(128)}, f32[32]{0:T(128)}, f32[32,256,512]{2,1,0:T(8,128)S(1)}, f32[32,256,512]{2,1,0:T(8,128)}) fusion(f32[32,256,512]{2,1,0:T(8,128)} %param.7, f32[32,256,512]{2,1,0:T(8,128)} %param.8, f32[32]{0:T(128)S(1)} %copy-done.9, f32[32]{0:T(128)S(1)} %copy-done.7, f32[32,64,256]{2,1,0:T(8,128)} %all-gather.3.cloned.1.call-done, ...), kind=kOutput, calls=%fused_computation.205 | convolution fusion | flops 3330277376 | bytes 69337600 | tf_op jit(solution)/shard_map/ckh,wk->chw/dot_general | solution.py:143
  216.9 6.2 %copy-done.4 = f32[32,256,512]{2,1,0:T(8,128)} copy-done((f32[32,256,512]{2,1,0:T(8,128)}, f32[32,256,512]{2,1,0:T(8,128)S(1)}, u32[]{:S(2)}) %copy-start.4) | copy-done | bytes 16777240
  223.1 17.8 %convolution_bitcast_fusion = f32[32,64,256]{2,1,0:T(8,128)} fusion(f32[512,64,1]{0,1,2:T(8,128)S(1)} %reshape.294, f32[32,256,512]{2,1,0:T(8,128)S(1)} %get-tuple-element.9), kind=kOutput, calls=%fused_computation.34 | convolution fusion | flops 3221225472 | bytes 19005440 | tf_op jit(solution)/shard_map/chw,wk->ckh/dot_general | solution.py:128
  241.0 10.9 %reduce-scatter.12.cloned.1.call-done = f32[32,32,256]{2,1,0:T(8,128)} async-done(((f32[32,64,256]{2,1,0:T(8,128)}), f32[32,32,256]{2,1,0:T(8,128)}) %reduce-scatter.12.cloned.1.call-update) | async-done | bytes 1048592 | tf_op jit(solution)/shard_map/reduce_scatter | solution.py:129
  251.9 1.8 reshape.290
  260.1 21.4 %reduce-scatter.14.cloned.1.call-done = f32[512,2,16]{0,2,1:T(8,128)} async-done(((f32[512,2,64]{0,2,1:T(8,128)}), f32[512,2,16]{0,2,1:T(8,128)}) %reduce-scatter.14.cloned.1.call-update) | async-done | bytes 65552 | tf_op jit(solution)/shard_map/reduce_scatter | solution.py:131
  282.6 11.9 %all_gather.17 = f32[64,16,2,16]{1,0,3,2:T(8,128)S(1)} all-gather(f32[32,16,2,16]{1,0,3,2:T(8,128)S(1)} %broadcast_multiply_fusion.1), channel_id=1, replica_groups=mesh['member'=2,'slab'=4,'chan'=2,'mode'=2] {'chan'}, dimensions={0}, use_global_device_ids=true | all-gather | bytes 196608 | tf_op jit(solution)/shard_map/all_gather | solution.py:163
  295.0 11.1 %fusion.16 = f32[16,16,1,32]{3,2,1,0:T(1,128)S(1)} fusion(f32[64,16,16,1]{0,3,2,1:T(1,128)S(1)} %copy.64, f32[32,64,16,16]{1,3,2,0:T(8,128)} %get-tuple-element.11), kind=kOutput, calls=%fused_computation.28 | convolution fusion | flops 6291456 | bytes 2195456 | tf_op jit(solution)/shard_map/oyx,ioyx->iyx/dot_general | solution.py:72
  306.0 10.9 %fusion.6 = f32[16,16,1,32]{3,2,1,0:T(1,128)S(1)} fusion(f32[64,16,16,1]{0,3,2,1:T(1,128)S(1)} %copy.64, f32[32,64,16,16]{1,3,2,0:T(8,128)} %get-tuple-element.12), kind=kOutput, calls=%fused_computation.18 | convolution fusion | flops 6291456 | bytes 2195456 | tf_op jit(solution)/shard_map/oyx,ioyx->iyx/dot_general | solution.py:75
  317.1 11.1 %fusion.14 = f32[16,16,1,32]{3,2,1,0:T(1,128)S(1)} fusion(f32[64,16,16,1]{0,3,2,1:T(1,128)S(1)} %copy.66, f32[32,64,16,16]{1,3,2,0:T(8,128)} %get-tuple-element.11), kind=kOutput, calls=%fused_computation.26 | convolution fusion | flops 6291456 | bytes 2195456 | tf_op jit(solution)/shard_map/oyx,ioyx->iyx/dot_general | solution.py:75
  328.2 10.9 %fusion.8 = f32[16,16,1,32]{3,2,1,0:T(1,128)S(1)} fusion(f32[64,16,16,1]{0,3,2,1:T(1,128)S(1)} %copy.66, f32[32,64,16,16]{1,3,2,0:T(8,128)} %get-tuple-element.12), kind=kOutput, calls=%fused_computation.20 | convolution fusion | flops 6291456 | bytes 2195456 | tf_op jit(solution)/shard_map/oyx,ioyx->iyx/dot_general | solution.py:72
  339.3 19.9 %all_gather.18 = f32[32,16,2,64]{0,1,2,3:T(8,128)S(1)} all-gather(f32[32,16,2,16]{0,1,2,3:T(8,128)S(1)} %pad_maximum_fusion.5), channel_id=1, replica_groups=mesh['member'=2,'slab'=4,'chan'=2,'mode'=2] {'slab'}, dimensions={3}, use_global_device_ids=true | all-gather | bytes 327680 | tf_op jit(solution)/shard_map/all_gather | solution.py:137
  365.5 1.7 reshape.293
  367.7 14.5 %all-reduce = (f32[32]{0:T(128)}, f32[32]{0:T(128)}) all-reduce(f32[32]{0:T(128)} %get-tuple-element.6, f32[32]{0:T(128)S(1)} %copy-done.10), channel_id=1, replica_groups=mesh['member'=2,'slab'=4,'chan'=2,'mode'=2] {'slab','mode'}, use_global_device_ids=true, to_apply=%region_6.7 | all-reduce | flops 64 | bytes 512 | tf_op jit(solution)/shard_map/psum | solution.py:166
  382.6 2.3 add_bitcast_fusion
  385.0 4.5 %maximum_multiply_fusion = f32[32,64,16,2,16]{1,4,3,2,0:T(8,128)} fusion(f32[32,64,16,1,16]{1,4,3,2,0:T(8,128)S(1)} %get-tuple-element.22, f32[32,64,16,1,16]{1,4,3,2,0:T(8,128)S(1)} %get-tuple-element.21, f32[32,64]{1,0:T(8,128)S(1)} %copy-done.6), kind=kLoop, calls=%fused_computation.12 | loop fusion | flops 2097152 | bytes 8396800 | tf_op jit(solution)/shard_map/mul | solution.py:164
  389.5 21.3 %multiply_add_fusion = f32[32,256,512]{2,1,0:T(8,128)} fusion(f32[32,256,512]{2,1,0:T(8,128)} %copy-done.4, f32[32,64,256]{2,1,0:T(8,128)} %all-gather.5.cloned.1.call-done, f32[512,64,1]{0,1,2:T(8,128)S(1)} %reshape.294, f32[32]{0:T(128)S(1)} %copy-done.7), kind=kOutput, calls=%fused_computation.9 | convolution fusion | flops 3229614080 | bytes 35782784 | tf_op jit(solution)/shard_map/ckh,wk->chw/dot_general | solution.py:143
  (98 shorter events, 33.3 us)
Async XLA Ops:
  7.2 21.7 %copy-start = (s32[64,2]{0,1:T(2,128)S(1)}, s32[64,2]{0,1:T(2,128)}, u32[]{:S(2)}) copy-start(s32[64,2]{0,1:T(2,128)} %param.12) | copy-start | bytes 1540
  7.2 33.9 %reduce-scatter.6.cloned.1.call-start = ((), (), s32[]{:S(2)}) async-start(), calls=%async_computation.5 | async-start | bytes 3145728 | tf_op jit(solution)/shard_map/reduce_scatter | solution.py:129
  7.8 21.3 %copy-start.8 = (s32[64]{0:T(128)S(1)}, s32[64]{0:T(128)}, u32[]{:S(2)}) copy-start(s32[64]{0:T(128)} %param.13) | copy-start | bytes 772
  28.5 42.1 %reduce-scatter.8.cloned.1.call-start = ((), (), s32[]{:S(2)}) async-start(), calls=%async_computation.6 | async-start | bytes 327680 | tf_op jit(solution)/shard_map/reduce_scatter | solution.py:131
  29.2 0.6 copy-start.5
  49.2 72.4 %reduce-scatter.10.cloned.1.call-start = ((), (), s32[]{:S(2)}) async-start(), calls=%async_computation.7 | async-start | bytes 1572864 | tf_op jit(solution)/shard_map/reduce_scatter | solution.py:154
  72.1 17.0 %copy-start.3 = (f32[32,64,16,16]{1,3,2,0:T(8,128)S(1)}, f32[32,64,16,16]{1,3,2,0:T(8,128)}, u32[]{:S(2)}) copy-start(f32[32,64,16,16]{1,3,2,0:T(8,128)} %get-tuple-element.11) | copy-start | bytes 6291460
  72.1 23.1 %copy-start.2 = (f32[32,64,16,16]{1,3,2,0:T(8,128)S(1)}, f32[32,64,16,16]{1,3,2,0:T(8,128)}, u32[]{:S(2)}) copy-start(f32[32,64,16,16]{1,3,2,0:T(8,128)} %get-tuple-element.12) | copy-start | bytes 6291460
  102.8 78.0 %all-gather.3.cloned.1.call-start = ((), (), s32[]{:S(2)}) async-start(), calls=%async_computation.8 | async-start | bytes 3145728 | tf_op jit(solution)/shard_map/all_gather | solution.py:142
  122.7 58.1 %copy-start.7 = (f32[32]{0:T(128)S(1)}, f32[32]{0:T(128)}, u32[]{:S(2)}) copy-start(f32[32]{0:T(128)} %param.10) | copy-start | bytes 388
  122.7 58.1 %copy-start.9 = (f32[32]{0:T(128)S(1)}, f32[32]{0:T(128)}, u32[]{:S(2)}) copy-start(f32[32]{0:T(128)} %param.11) | copy-start | bytes 388
  169.7 82.2 %reduce-scatter.12.cloned.1.call-start = ((), (), s32[]{:S(2)}) async-start(), calls=%async_computation.9 | async-start | bytes 3145728 | tf_op jit(solution)/shard_map/reduce_scatter | solution.py:129
  216.9 6.2 %copy-start.4 = (f32[32,256,512]{2,1,0:T(8,128)}, f32[32,256,512]{2,1,0:T(8,128)S(1)}, u32[]{:S(2)}) copy-start(f32[32,256,512]{2,1,0:T(8,128)S(1)} %get-tuple-element.9) | copy-start | bytes 50331652
  240.9 40.6 %reduce-scatter.14.cloned.1.call-start = ((), (), s32[]{:S(2)}) async-start(), calls=%async_computation.10 | async-start | bytes 327680 | tf_op jit(solution)/shard_map/reduce_scatter | solution.py:131
  260.0 129.5 %all-gather.5.cloned.1.call-start = ((), (), s32[]{:S(2)}) async-start(), calls=%async_computation.11 | async-start | bytes 3145728 | tf_op jit(solution)/shard_map/all_gather | solution.py:142
  339.1 28.6 %copy-start.10 = (f32[32]{0:T(128)S(1)}, f32[32]{0:T(128)}, u32[]{:S(2)}) copy-start(f32[32]{0:T(128)} %get-tuple-element.5) | copy-start | bytes 388
  364.7 20.2 %copy-start.6 = (f32[32,64]{1,0:T(8,128)S(1)}, f32[32,64]{1,0:T(8,128)}, u32[]{:S(2)}) copy-start(f32[32,64]{1,0:T(8,128)} %copy-done.5) | copy-start | bytes 24580
  389.5 21.3 %copy-start.1 = (s32[64,2]{0,1:T(2,128)S(1)}, s32[64,2]{0,1:T(2,128)}, u32[]{:S(2)}) copy-start(s32[64,2]{0,1:T(2,128)} %param.12) | copy-start | bytes 1540
Sparse Core Ops, SparseCore 0:
  28.6 12.3 reduce-scatter.5
  49.3 21.2 reduce-scatter.7
  103.0 18.5 reduce-scatter.9
  169.8 11.0 all-gather.2
  241.0 10.7 reduce-scatter.11
  260.1 21.2 reduce-scatter.13
  367.4 10.3 all-gather.4
where the time goes:
time: 424 us; the launch traced here: 418 us
  matrix products  188 us (44%)
  blocking collectives  84.8 us (20%)
  waiting for transfers between devices  78.2 us (18%)
  local copies, waits for them, and re-layouts  32.6 us (8%)
  other arithmetic  19.1 us (5%)
  between operations  15.1 us (4%)
    all_gather x2, blocking collectives, synthesis(): whole_modes = lax.all_gather(modes_in, 'slab', axis=3, tiled=True)  58.4 us
    dot_general x2, matrix products, synthesis(): return jnp.einsum('ckh,wk->chw', gathered, column_tab, precision=precise)  57.4 us
    dot_general x2, matrix products, spectrum(): jnp.einsum('chw,wk->ckh', values, column_tab, precision=precise)  38.5 us
    reduce_scatter x2, waiting for transfers between devices, spectrum(): lax.psum_scatter(row_forward(paired, row_cos, row_sin), 'slab', scatter_d...  34.8 us
    reduce_scatter x1, waiting for transfers between devices, local(): lax.psum_scatter(contract(spectra, masked_weight), 'chan', scatter_dimens...  18.5 us
    psum x1, blocking collectives, local(): lax.psum((jnp.sum(grad_sum * source_field, axis=(1, 2)), jnp.sum(grad_sum...  14.5 us
    reduce_scatter x2, waiting for transfers between devices, spectrum(): lax.psum_scatter(partial_cols, 'mode', scatter_dimension=1, tiled=True)  13.6 us
    all_gather x1, blocking collectives, local(): all_grads = lax.all_gather(grad_modes, 'chan', axis=0, tiled=True)  11.9 us
  transfers between devices with their start and end apart: 7, of which 6 were waited for; matrix products, arithmetic and copies ran while one was open for 6% of the time, Pallas kernels for 0%

commit v1 on v0

--- a/solution.py
+++ b/solution.py
@@ -134,7 +134,7 @@
         return spectra.reshape(values.shape[0], local_freq, 2, local_kx)
 
     def synthesis(modes_in):
-        whole_modes = lax.all_gather(modes_in, "slab", axis=3, tiled=True)
+        whole_modes = jnp.concatenate(lax.all_gather(modes_in, "slab"), axis=3)
         rebuilt = row_inverse(
             whole_modes.reshape(channels * local_freq, 2, kx_count), row_cos, row_sin
         )

time: 424 us -> 409 us (0.965)
  matrix products: 188 us -> 144 us
  blocking collectives: 84.8 us -> 99.6 us
  other arithmetic: 19.1 us -> 30.9 us
    dot_general x4 -> x0, matrix products: 43.9 us -> none  [the longest x1 11.1 us: contract_back(): jnp.einsum('oyx,ioyx->iyx', grad_imag, weight_real, precision=precise)]
    all_gather x2, blocking collectives: 58.4 us -> 73.3 us  [synthesis(): whole_modes = jnp.concatenate(lax.all_gather(modes_in, 'slab'), axis=3)]
    another operation x1, other arithmetic: 2.33 us -> 10.6 us  [outer_grad(): return jnp.stack([real_side, imag_side], axis=3)]
where the time goes in v1:
time: 409 us; the launch traced here: 404 us
  matrix products  144 us (35%)
  blocking collectives  99.6 us (24%)
  waiting for transfers between devices  78.4 us (19%)
  local copies, waits for them, and re-layouts  35.6 us (9%)
  other arithmetic  30.9 us (8%)
  between operations  14.8 us (4%)
    all_gather x2, blocking collectives, synthesis(): whole_modes = jnp.concatenate(lax.all_gather(modes_in, 'slab'), axis=3)  73.3 us
    dot_general x2, matrix products, synthesis(): return jnp.einsum('ckh,wk->chw', gathered, column_tab, precision=precise)  57.5 us
    dot_general x2, matrix products, spectrum(): jnp.einsum('chw,wk->ckh', values, column_tab, precision=precise)  38.3 us
    reduce_scatter x2, waiting for transfers between devices, spectrum(): lax.psum_scatter(row_forward(paired, row_cos, row_sin), 'slab', scatter_d...  34.3 us
    reduce_scatter x1, waiting for transfers between devices, local(): lax.psum_scatter(contract(spectra, masked_weight), 'chan', scatter_dimens...  18.5 us
    psum x1, blocking collectives, local(): lax.psum((jnp.sum(grad_sum * source_field, axis=(1, 2)), jnp.sum(grad_sum...  14.4 us
    reduce_scatter x2, waiting for transfers between devices, spectrum(): lax.psum_scatter(partial_cols, 'mode', scatter_dimension=1, tiled=True)  14.3 us
    all_gather x1, blocking collectives, local(): all_grads = lax.all_gather(grad_modes, 'chan', axis=0, tiled=True)  11.9 us
  transfers between devices with their start and end apart: 7, of which 6 were waited for; matrix products, arithmetic and copies ran while one was open for 6% of the time, Pallas kernels for 0%

profile of v1, /device:TPU:0, one launch (start us, length us, event | category | flops | bytes accessed | tf_op | source)
XLA Modules:
  0.0 403.7 jit_solution(15987355409895090514)
XLA Ops:
  7.8 20.7 %convolution_bitcast_fusion.1 = f32[32,64,256]{2,1,0:T(8,128)} fusion(f32[512,64,1]{0,1,2:T(8,128)S(1)} %reshape.296, f32[32,256,512]{2,1,0:T(8,128)} %param.7), kind=kOutput, calls=%fused_computation.36 | convolution fusion | flops 3221225472 | bytes 19005440 | tf_op jit(solution)/shard_map/chw,wk->ckh/dot_general | solution.py:128
  29.1 8.5 %broadcast_multiply_fusion = f32[32,64,16,2,16]{1,4,3,2,0:T(8,128)} fusion(f32[32,64,16,2,16]{1,4,3,2,0:T(8,128)} %param.9, f32[32,64]{1,0:T(8,128)S(1)} %compare_convert_fusion), kind=kLoop, calls=%fused_computation.23 | loop fusion | flops 1048576 | bytes 8396800 | tf_op jit(solution)/shard_map/mul | solution.py:151
  37.6 3.4 reduce-scatter.6.cloned.1.call-done
  41.0 1.8 reshape.286
  49.5 7.9 %slice_bitcast_fusion.1 = (f32[32,64,16,16]{1,3,2,0:T(8,128)}, f32[32,64,16,16]{1,3,2,0:T(8,128)}) fusion(f32[32,64,16,2,16]{1,4,3,2,0:T(8,128)} %broadcast_multiply_fusion), kind=kLoop, calls=%fused_computation.33 | loop fusion | bytes 8388608 | tf_op jit(solution)/shard_map/squeeze | solution.py:56
  57.4 13.3 %reduce-scatter.8.cloned.1.call-done = f32[512,2,16]{0,2,1:T(8,128)} async-done(((f32[512,2,64]{0,2,1:T(8,128)}), f32[512,2,16]{0,2,1:T(8,128)}) %reduce-scatter.8.cloned.1.call-update) | async-done | bytes 65552 | tf_op jit(solution)/shard_map/reduce_scatter | solution.py:131
  72.8 8.3 %fusion.14 = f32[16,16,1,64]{3,2,1,0:T(1,128)S(1)} fusion(f32[32,16,16,1]{0,3,2,1:T(1,128)S(1)} %copy.72, f32[32,64,16,16]{1,3,2,0:T(8,128)} %get-tuple-element.17), kind=kOutput, calls=%fused_computation.28 | convolution fusion | flops 6291456 | bytes 2195456 | tf_op jit(solution)/shard_map/iyx,ioyx->oyx/dot_general | solution.py:61
  81.2 8.6 %fusion.16 = f32[16,16,1,64]{3,2,1,0:T(1,128)S(1)} fusion(f32[32,16,16,1]{0,3,2,1:T(1,128)S(1)} %copy.69, f32[32,64,16,16]{1,3,2,0:T(8,128)} %get-tuple-element.17), kind=kOutput, calls=%fused_computation.30 | convolution fusion | flops 6291456 | bytes 2195456 | tf_op jit(solution)/shard_map/iyx,ioyx->oyx/dot_general | solution.py:58
  89.8 6.0 %fusion.10 = f32[16,16,1,64]{3,2,1,0:T(1,128)S(1)} fusion(f32[32,16,16,1]{0,3,2,1:T(1,128)S(1)} %copy.69, f32[32,64,16,16]{1,3,2,0:T(8,128)S(1)} %copy-done.3), kind=kOutput, calls=%fused_computation.24 | convolution fusion | flops 6291456 | bytes 2195456 | tf_op jit(solution)/shard_map/iyx,ioyx->oyx/dot_general | solution.py:61
  95.9 6.2 %fusion.12 = f32[16,16,1,64]{3,2,1,0:T(1,128)S(1)} fusion(f32[32,16,16,1]{0,3,2,1:T(1,128)S(1)} %copy.72, f32[32,64,16,16]{1,3,2,0:T(8,128)S(1)} %copy-done.3), kind=kOutput, calls=%fused_computation.26 | convolution fusion | flops 6291456 | bytes 2195456 | tf_op jit(solution)/shard_map/iyx,ioyx->oyx/dot_general | solution.py:58
  102.2 1.3 copy.57
  103.7 18.5 %reduce-scatter.10.cloned.1.call-done = f32[32,16,2,16]{1,0,3,2:T(8,128)} async-done(((f32[64,16,2,16]{1,0,3,2:T(8,128)}), f32[32,16,2,16]{1,0,3,2:T(8,128)}) %reduce-scatter.10.cloned.1.call-update) | async-done | bytes 65552 | tf_op jit(solution)/shard_map/reduce_scatter | solution.py:154
  123.4 38.3 %all-gather = f32[128,16,2,16]{1,0,3,2:T(8,128)S(1)} all-gather(f32[32,16,2,16]{1,0,3,2:T(8,128)S(1)} %broadcast_multiply_fusion.2), channel_id=2, replica_groups=mesh['member'=2,'slab'=4,'chan'=2,'mode'=2] {'slab'}, dimensions={0}, use_global_device_ids=true | all-gather | bytes 327680 | tf_op jit(solution)/shard_map/all_gather | solution.py:137
  162.0 1.6 reshape_reshape.6
  169.0 1.7 reshape.289
  170.8 11.1 %all-gather.5.cloned.1.call-done = f32[32,64,256]{2,1,0:T(8,128)} async-done(((f32[32,32,256]{2,1,0:T(8,128)}), f32[32,64,256]{2,1,0:T(8,128)}) %all-gather.5.cloned.1.call-update) | async-done | bytes 2097168 | tf_op jit(solution)/shard_map/all_gather | solution.py:142
  181.9 36.3 %fusion.144 = (f32[32]{0:T(128)}, f32[32]{0:T(128)}, f32[32,256,512]{2,1,0:T(8,128)S(1)}, f32[32,256,512]{2,1,0:T(8,128)}) fusion(f32[32,256,512]{2,1,0:T(8,128)} %param.7, f32[32,256,512]{2,1,0:T(8,128)} %param.8, f32[32]{0:T(128)S(1)} %copy-done.9, f32[32]{0:T(128)S(1)} %copy-done.7, f32[32,64,256]{2,1,0:T(8,128)} %all-gather.5.cloned.1.call-done, ...), kind=kOutput, calls=%fused_computation.202 | convolution fusion | flops 3330277376 | bytes 69337600 | tf_op jit(solution)/shard_map/ckh,wk->chw/dot_general | solution.py:143
  218.2 6.2 %copy-done.2 = f32[32,256,512]{2,1,0:T(8,128)} copy-done((f32[32,256,512]{2,1,0:T(8,128)}, f32[32,256,512]{2,1,0:T(8,128)S(1)}, u32[]{:S(2)}) %copy-start.2) | copy-done | bytes 16777240
  224.4 17.6 %convolution_bitcast_fusion = f32[32,64,256]{2,1,0:T(8,128)} fusion(f32[512,64,1]{0,1,2:T(8,128)S(1)} %reshape.296, f32[32,256,512]{2,1,0:T(8,128)S(1)} %get-tuple-element.15), kind=kOutput, calls=%fused_computation.35 | convolution fusion | flops 3221225472 | bytes 19005440 | tf_op jit(solution)/shard_map/chw,wk->ckh/dot_general | solution.py:128
  242.0 10.9 %reduce-scatter.12.cloned.1.call-done = f32[32,32,256]{2,1,0:T(8,128)} async-done(((f32[32,64,256]{2,1,0:T(8,128)}), f32[32,32,256]{2,1,0:T(8,128)}) %reduce-scatter.12.cloned.1.call-update) | async-done | bytes 1048592 | tf_op jit(solution)/shard_map/reduce_scatter | solution.py:129
  252.9 1.8 reshape.290
  259.1 1.2 fusion.22
  261.5 21.0 %reduce-scatter.14.cloned.1.call-done = f32[512,2,16]{0,2,1:T(8,128)} async-done(((f32[512,2,64]{0,2,1:T(8,128)}), f32[512,2,16]{0,2,1:T(8,128)}) %reduce-scatter.14.cloned.1.call-update) | async-done | bytes 65552 | tf_op jit(solution)/shard_map/reduce_scatter | solution.py:131
  283.6 11.9 %all_gather.24 = f32[64,16,2,16]{1,0,3,2:T(8,128)S(1)} all-gather(f32[32,16,2,16]{1,0,3,2:T(8,128)S(1)} %broadcast_multiply_fusion.1), channel_id=1, replica_groups=mesh['member'=2,'slab'=4,'chan'=2,'mode'=2] {'chan'}, dimensions={0}, use_global_device_ids=true | all-gather | bytes 196608 | tf_op jit(solution)/shard_map/all_gather | solution.py:163
  296.0 10.6 %add_bitcast_fusion = (f32[32,64,16,1,16]{1,4,3,2,0:T(8,128)}, f32[32,64,16,1,16]{1,4,3,2,0:T(8,128)}, f32[16,16,32]{1,0,2:T(8,128)S(1)}, f32[16,16,32]{1,0,2:T(...) fusion(f32[16,16,64]{2,1,0:T(8,128)S(1)} %copy.106, f32[16,16,64]{2,1,0:T(8,128)S(1)} %copy.105, ...), kind=kLoop, calls=%fused_computation.22 | loop fusion | flops 7307264 | bytes 8716288 | tf_op jit(solution)/shard_map/stack | solution.py:92
  306.7 35.0 %all-gather.1 = f32[128,16,2,16]{3,1,2,0:T(8,128)S(1)} all-gather(f32[32,16,2,16]{3,1,2,0:T(8,128)S(1)} %pad_maximum_fusion.2), channel_id=3, replica_groups=mesh['member'=2,'slab'=4,'chan'=2,'mode'=2] {'slab'}, dimensions={0}, use_global_device_ids=true | all-gather | bytes 327680 | tf_op jit(solution)/shard_map/all_gather | solution.py:137
  341.7 1.3 copy.100
  343.9 1.6 reshape_reshape.7
  351.0 1.7 reshape.293
  352.7 14.4 %all-reduce = (f32[32]{0:T(128)}, f32[32]{0:T(128)}) all-reduce(f32[32]{0:T(128)S(1)} %copy-done.11, f32[32]{0:T(128)S(1)} %copy-done.10), channel_id=1, replica_groups=mesh['member'=2,'slab'=4,'chan'=2,'mode'=2] {'slab','mode'}, use_global_device_ids=true, to_apply=%region_6.7 | all-reduce | flops 64 | bytes 512 | tf_op jit(solution)/shard_map/psum | solution.py:166
  367.1 8.2 %maximum_multiply_fusion = f32[32,64,16,2,16]{1,4,3,2,0:T(8,128)} fusion(f32[32,64,16,1,16]{1,4,3,2,0:T(8,128)} %get-tuple-element.26, f32[32,64,16,1,16]{1,4,3,2,0:T(8,128)} %get-tuple-element.25, f32[32,64]{1,0:T(8,128)S(1)} %copy-done.6), kind=kLoop, calls=%fused_computation.12 | loop fusion | flops 2097152 | bytes 8396800 | tf_op jit(solution)/shard_map/mul | solution.py:164
  375.3 21.3 %multiply_add_fusion = f32[32,256,512]{2,1,0:T(8,128)} fusion(f32[32,256,512]{2,1,0:T(8,128)} %copy-done.2, f32[32,64,256]{2,1,0:T(8,128)} %all-gather.7.cloned.1.call-done, f32[512,64,1]{0,1,2:T(8,128)S(1)} %reshape.296, f32[32]{0:T(128)S(1)} %copy-done.7), kind=kOutput, calls=%fused_computation.9 | convolution fusion | flops 3229614080 | bytes 35782784 | tf_op jit(solution)/shard_map/ckh,wk->chw/dot_general | solution.py:143
  (97 shorter events, 30.5 us)
Async XLA Ops:
  7.2 21.6 %copy-start = (s32[64,2]{0,1:T(2,128)S(1)}, s32[64,2]{0,1:T(2,128)}, u32[]{:S(2)}) copy-start(s32[64,2]{0,1:T(2,128)} %param.12) | copy-start | bytes 1540
  7.2 33.9 %reduce-scatter.6.cloned.1.call-start = ((), (), s32[]{:S(2)}) async-start(), calls=%async_computation.5 | async-start | bytes 3145728 | tf_op jit(solution)/shard_map/reduce_scatter | solution.py:129
  7.8 21.3 %copy-start.8 = (s32[64]{0:T(128)S(1)}, s32[64]{0:T(128)}, u32[]{:S(2)}) copy-start(s32[64]{0:T(128)} %param.13) | copy-start | bytes 772
  28.5 42.1 %reduce-scatter.8.cloned.1.call-start = ((), (), s32[]{:S(2)}) async-start(), calls=%async_computation.6 | async-start | bytes 327680 | tf_op jit(solution)/shard_map/reduce_scatter | solution.py:131
  29.1 8.5 %copy-start.5 = (f32[32,64]{1,0:T(8,128)}, f32[32,64]{1,0:T(8,128)S(1)}, u32[]{:S(2)}) copy-start(f32[32,64]{1,0:T(8,128)S(1)} %compare_convert_fusion) | copy-start | bytes 24580
  49.2 73.1 %reduce-scatter.10.cloned.1.call-start = ((), (), s32[]{:S(2)}) async-start(), calls=%async_computation.7 | async-start | bytes 1572864 | tf_op jit(solution)/shard_map/reduce_scatter | solution.py:154
  72.8 17.0 %copy-start.3 = (f32[32,64,16,16]{1,3,2,0:T(8,128)S(1)}, f32[32,64,16,16]{1,3,2,0:T(8,128)}, u32[]{:S(2)}) copy-start(f32[32,64,16,16]{1,3,2,0:T(8,128)} %get-tuple-element.18) | copy-start | bytes 6291460
  103.5 78.4 %all-gather.5.cloned.1.call-start = ((), (), s32[]{:S(2)}) async-start(), calls=%async_computation.8 | async-start | bytes 3145728 | tf_op jit(solution)/shard_map/all_gather | solution.py:142
  161.8 20.2 %copy-start.7 = (f32[32]{0:T(128)S(1)}, f32[32]{0:T(128)}, u32[]{:S(2)}) copy-start(f32[32]{0:T(128)} %param.10) | copy-start | bytes 388
  161.8 20.2 %copy-start.9 = (f32[32]{0:T(128)S(1)}, f32[32]{0:T(128)}, u32[]{:S(2)}) copy-start(f32[32]{0:T(128)} %param.11) | copy-start | bytes 388
  170.7 82.2 %reduce-scatter.12.cloned.1.call-start = ((), (), s32[]{:S(2)}) async-start(), calls=%async_computation.9 | async-start | bytes 3145728 | tf_op jit(solution)/shard_map/reduce_scatter | solution.py:129
  218.2 6.2 %copy-start.2 = (f32[32,256,512]{2,1,0:T(8,128)}, f32[32,256,512]{2,1,0:T(8,128)S(1)}, u32[]{:S(2)}) copy-start(f32[32,256,512]{2,1,0:T(8,128)S(1)} %get-tuple-element.15) | copy-start | bytes 50331652
  241.9 19.2 %copy-start.4 = (f32[16,16,32]{0,2,1:T(8,128)S(1)}, f32[16,16,32]{0,2,1:T(8,128)}, u32[]{:S(2)}) copy-start(f32[16,16,32]{0,2,1:T(8,128)} %get-tuple-element.27) | copy-start | bytes 98308
  242.0 40.6 %reduce-scatter.14.cloned.1.call-start = ((), (), s32[]{:S(2)}) async-start(), calls=%async_computation.10 | async-start | bytes 327680 | tf_op jit(solution)/shard_map/reduce_scatter | solution.py:131
  261.1 114.2 %all-gather.7.cloned.1.call-start = ((), (), s32[]{:S(2)}) async-start(), calls=%async_computation.11 | async-start | bytes 3145728 | tf_op jit(solution)/shard_map/all_gather | solution.py:142
  343.1 9.7 %copy-start.10 = (f32[32]{0:T(128)S(1)}, f32[32]{0:T(128)}, u32[]{:S(2)}) copy-start(f32[32]{0:T(128)} %get-tuple-element.5) | copy-start | bytes 388
  343.1 9.7 %copy-start.11 = (f32[32]{0:T(128)S(1)}, f32[32]{0:T(128)}, u32[]{:S(2)}) copy-start(f32[32]{0:T(128)} %get-tuple-element.6) | copy-start | bytes 388
  343.1 24.0 %copy-start.6 = (f32[32,64]{1,0:T(8,128)S(1)}, f32[32,64]{1,0:T(8,128)}, u32[]{:S(2)}) copy-start(f32[32,64]{1,0:T(8,128)} %copy-done.5) | copy-start | bytes 24580
  375.3 21.3 %copy-start.1 = (s32[64,2]{0,1:T(2,128)S(1)}, s32[64,2]{0,1:T(2,128)}, u32[]{:S(2)}) copy-start(s32[64,2]{0,1:T(2,128)} %param.12) | copy-start | bytes 1540
Sparse Core Ops, SparseCore 0:
  28.6 12.3 reduce-scatter.5
  49.3 21.2 reduce-scatter.7
  103.7 18.5 reduce-scatter.9
  170.9 11.0 all-gather.4
  242.1 10.7 reduce-scatter.11
  261.2 21.2 reduce-scatter.13
  352.8 10.4 all-gather.6
